TPU v7x, 128 devices: a whole 4x4x4 slice. The times are simulated.
128 devices in a mesh: row: 16 (over x_hi, y, core), col: 4 (over z), dp: 2 (over x_lo).
Axes of the slice: x: 4 (x_hi: 2, x_lo: 2; x = x_hi * 2 + x_lo), y: 4, z: 4, core: 2. Of those that a mesh axis runs over, the one named last changes fastest.
Arguments:
- slides: bfloat16 [2, 256, 128, 512], P('dp', 'row', 'col'), may hold values from -6 to 6
- cotangent: bfloat16 [2, 256, 128, 512], P('dp', 'row', 'col'), may hold values from -6 to 6
- kernel: float32 [2, 7, 7, 512], replicated, may hold values from -0.875 to 0.875
- kernel_bias: float32 [2, 512], replicated, may hold values from -3 to 3
- norm_gain: float32 [2, 512], replicated, may hold values from 0.1 to 1.9
- norm_bias: float32 [2, 512], replicated, may hold values from -3 to 3
- weight_in: bfloat16 [2, 512, 2048], P(None, 'dp'), may hold values from -0.25 to 0.25
- bias_in: float32 [2, 2048], replicated, may hold values from -3 to 3
- weight_out: bfloat16 [2, 2048, 512], P(None, None, 'dp'), may hold values from -0.125 to 0.125
- bias_out: float32 [2, 512], replicated, may hold values from -3 to 3
- layer_scale: float32 [2, 512], replicated, may hold values from 0.3 to 1.5
Outputs:
- output: bfloat16 [2, 256, 128, 512], P('dp', 'row', 'col')
- grad_slides: bfloat16 [2, 256, 128, 512], P('dp', 'row', 'col')
- grad_weight_in: float32 [2, 512, 2048], P(None, 'dp')
- grad_weight_out: float32 [2, 2048, 512], P(None, None, 'dp')
- grad_kernel: float32 [2, 7, 7, 512], replicated
- grad_channel: float32 [2, 5, 512], replicated
- grad_bias_in: float32 [2, 2048], replicated
All inputs are finite; a program needn't handle non-finite values.
Results may differ from a plain program's by a relative error of at most 0.01.
Values may be sent and summed in bfloat16 or wider, within the bound.
No kernel may reach another device: no remote copies, remote signals or barrier semaphores. Data moves between devices by JAX's collectives and lax.ppermute only.
A program may use at most 128 MiB of HBM per device.

v0:
```python
import jax
import jax.numpy as jnp
from jax import lax
from jax.sharding import PartitionSpec as P

COEF = 0.7978845608028654
CUBIC = 0.044715
EPSILON = 1e-06


def cut_along(shard, dim, size):
    before, after = (shard.shape[:dim], shard.shape[dim + 1 :])
    return jnp.moveaxis(shard.reshape(*before, size, -1, *after), dim, 0)


def sent_and_summed(shard, axis, dim):
    size = lax.axis_size(axis)
    pieces = lax.all_to_all(cut_along(shard, dim, size), axis, 0, 0, tiled=True)
    return jnp.sum(pieces.astype(jnp.float32), axis=0)


def padded_to(lines, size):
    spare = -len(lines) % size
    return jnp.pad(lines, [(0, spare)] + [(0, 0)] * (lines.ndim - 1))


def copy_for_each(shard, axis):
    copies = jnp.broadcast_to(shard, (lax.axis_size(axis), *shard.shape))
    return lax.all_to_all(copies, axis, split_axis=0, concat_axis=0, tiled=True)


def in_order(pieces, dim):
    pieces = jnp.moveaxis(pieces, 0, dim)
    lengths = pieces.shape
    return pieces.reshape(*lengths[:dim], lengths[dim] * lengths[dim + 1], *lengths[dim + 2 :])


def gather_directly(shard, axis, dim):
    pieces = copy_for_each(shard, axis)
    return in_order(pieces, dim)


def total_of(shard, axes):
    lines = shard.reshape(-1, shard.shape[-1])
    padded = padded_to(lines, lax.axis_size(axes))
    whole = gather_directly(sent_and_summed(padded, axes, 0).astype(jnp.bfloat16), axes, 0)
    return lax.slice_in_dim(whole, 0, len(lines)).reshape(shard.shape).astype(jnp.float32)


def turned_gather(arrays, axis, dims):
    turned = [jnp.moveaxis(a, dim, 0) for a, dim in zip(arrays, dims)]
    widths = [t[0].size for t in turned]
    both = jnp.concatenate([t.reshape(-1, w) for t, w in zip(turned, widths)], axis=1)
    result = lax.all_gather(both, axis, axis=0, tiled=True)
    pieces = jnp.split(result, [sum(widths[:k]) for k in range(1, len(widths))], axis=1)
    return tuple(
        (
            jnp.moveaxis(b.reshape(-1, *t.shape[1:]), 0, dim)
            for b, t, dim in zip(pieces, turned, dims)
        )
    )


def with_halo(block, sides, width):
    for axis, dim in sides:
        count = lax.axis_size(axis)
        forward = [(i, i + 1) for i in range(count - 1)]
        backward = [(target, source) for source, target in forward]
        low = lax.ppermute(
            lax.slice_in_dim(block, block.shape[dim] - width, None, axis=dim), axis, forward
        )
        high = lax.ppermute(lax.slice_in_dim(block, 0, width, axis=dim), axis, backward)
        block = jnp.concatenate([low, block, high], axis=dim)
    return block


def gelu_tanh(values):
    inner = COEF * (values + CUBIC * values * values * values)
    return 0.5 * values * (1.0 + jnp.tanh(inner))


def gelu_slope(values):
    tangent = jnp.tanh(COEF * (values + CUBIC * values * values * values))
    return 0.5 * (1.0 + tangent) + 0.5 * values * (1.0 - tangent * tangent) * COEF * (
        1.0 + 3.0 * CUBIC * values * values
    )


def depthwise(padded, taps):
    height = padded.shape[1] - 6
    width = padded.shape[2] - 6
    total = jnp.zeros((padded.shape[0], height, width, padded.shape[3]), jnp.float32)
    for row_tap in range(7):
        for col_tap in range(7):
            window = padded[:, row_tap : row_tap + height, col_tap : col_tap + width, :].astype(
                jnp.float32
            )
            total = total + window * taps[row_tap, col_tap]
    return total


def tap_grads(padded, upstream):
    height = upstream.shape[1]
    width = upstream.shape[2]
    rows_out = []
    for row_tap in range(7):
        line = []
        for col_tap in range(7):
            window = padded[:, row_tap : row_tap + height, col_tap : col_tap + width, :].astype(
                jnp.float32
            )
            line.append(jnp.sum(window * upstream, axis=(0, 1, 2)))
        rows_out.append(jnp.stack(line))
    return jnp.stack(rows_out)


def forward_layer(
    padded, current, taps, tap_bias, gain, shift, weight_in, bias_in, weight_out, bias_out, scale
):
    channels = current.shape[-1]
    mixed = (depthwise(padded, taps) + tap_bias).reshape(-1, channels)
    center = mixed - jnp.mean(mixed, -1, keepdims=True)
    rstd = lax.rsqrt(jnp.mean(center * center, -1, keepdims=True) + EPSILON)
    normed = center * rstd
    normal_low = (normed * gain + shift).astype(jnp.bfloat16)
    hidden = jnp.dot(normal_low, weight_in, preferred_element_type=jnp.float32) + bias_in
    activated = gelu_tanh(hidden).astype(jnp.bfloat16)
    branch = jnp.dot(activated, weight_out, preferred_element_type=jnp.float32) + bias_out
    result = current.reshape(-1, channels).astype(jnp.float32) + scale * branch
    result = result.astype(jnp.bfloat16).reshape(current.shape)
    return (result, (normed, rstd, normal_low, hidden, activated, branch))


def backward_layer(upstream, saved, gain, weight_in, weight_out, scale):
    normed, rstd, normal_low, hidden, activated, branch = saved
    contract_rows = (((0,), (0,)), ((), ()))
    contract_cols = (((1,), (1,)), ((), ()))
    grad_scale = jnp.sum(upstream * branch, 0)
    grad_branch = upstream * scale
    grad_bias_out = jnp.sum(grad_branch, 0)
    branch_low = grad_branch.astype(jnp.bfloat16)
    grad_weight_out = lax.dot_general(
        activated, branch_low, contract_rows, preferred_element_type=jnp.float32
    )
    grad_act = lax.dot_general(
        branch_low, weight_out, contract_cols, preferred_element_type=jnp.float32
    )
    grad_hidden = grad_act * gelu_slope(hidden)
    grad_bias_in = jnp.sum(grad_hidden, 0)
    hidden_low = grad_hidden.astype(jnp.bfloat16)
    grad_weight_in = lax.dot_general(
        normal_low, hidden_low, contract_rows, preferred_element_type=jnp.float32
    )
    grad_normal = lax.dot_general(
        hidden_low, weight_in, contract_cols, preferred_element_type=jnp.float32
    )
    grad_gain = jnp.sum(grad_normal * normed, 0)
    grad_shift = jnp.sum(grad_normal, 0)
    scaled = grad_normal * gain
    grad_mixed = rstd * (
        scaled
        - jnp.mean(scaled, -1, keepdims=True)
        - normed * jnp.mean(scaled * normed, -1, keepdims=True)
    )
    grad_tap_bias = jnp.sum(grad_mixed, 0)
    channel_grads = jnp.stack([grad_tap_bias, grad_gain, grad_shift, grad_bias_out, grad_scale])
    return (grad_mixed, grad_weight_in, grad_weight_out, grad_bias_in, channel_grads)


def reduce_weights(grad_in, grad_out):
    half_in, half_out = (
        sent_and_summed(grad_in.astype(jnp.bfloat16), "dp", 0),
        sent_and_summed(grad_out.astype(jnp.bfloat16), "dp", 1),
    )
    shard_in, shard_out = (
        total_of(half_in.astype(jnp.bfloat16), ("row", "col")),
        total_of(half_out.astype(jnp.bfloat16), ("row", "col")),
    )
    return (shard_in, shard_out)


def per_device(
    slides,
    cotangent,
    kernel,
    kernel_bias,
    norm_gain,
    norm_bias,
    weight_in,
    bias_in,
    weight_out,
    bias_out,
    layer_scale,
):
    layers = weight_in.shape[0]
    channels = slides.shape[-1]
    current = slides
    caches = []
    paddings = []
    fetched = []
    for which in range(layers):
        full_in, full_out = turned_gather((weight_in[which], weight_out[which]), "dp", (0, 1))
        fetched.append((full_in, full_out))
        padded = with_halo(current, (("row", 1), ("col", 2)), 3)
        current, cache = forward_layer(
            padded,
            current,
            kernel[which],
            kernel_bias[which],
            norm_gain[which],
            norm_bias[which],
            full_in,
            bias_in[which],
            full_out,
            bias_out[which],
            layer_scale[which],
        )
        caches.append(cache)
        paddings.append(padded)
    upstream = cotangent.astype(jnp.float32).reshape(-1, channels)
    grads_in = [None] * layers
    grads_out = [None] * layers
    grads_kernel = [None] * layers
    grads_channel = [None] * layers
    grads_bias = [None] * layers
    for which in reversed(range(layers)):
        full_in, full_out = fetched[which]
        grad_mixed, grad_in, grad_out, grad_bias, channel_grads = backward_layer(
            upstream, caches[which], norm_gain[which], full_in, full_out, layer_scale[which]
        )
        shaped = grad_mixed.reshape(slides.shape)
        rim = with_halo(shaped.astype(jnp.bfloat16), (("row", 1), ("col", 2)), 3).astype(
            shaped.dtype
        )
        local_taps = tap_grads(paddings[which], shaped)
        back = depthwise(rim, kernel[which][::-1, ::-1])
        upstream = upstream + back.reshape(-1, channels)
        grads_in[which], grads_out[which] = reduce_weights(grad_in, grad_out)
        grads_kernel[which], grads_channel[which], grads_bias[which] = lax.psum(
            (local_taps, channel_grads, grad_bias), ("row", "col", "dp")
        )
    grad_slides = upstream.astype(jnp.bfloat16).reshape(slides.shape)
    return (
        current,
        grad_slides,
        jnp.stack(grads_in),
        jnp.stack(grads_out),
        jnp.stack(grads_kernel),
        jnp.stack(grads_channel),
        jnp.stack(grads_bias),
    )


def solution(mesh):
    return jax.shard_map(
        per_device,
        mesh=mesh,
        in_specs=(
            P("dp", "row", "col", None),
            P("dp", "row", "col", None),
            P(),
            P(),
            P(),
            P(),
            P(None, "dp", None),
            P(),
            P(None, None, "dp"),
            P(),
            P(),
        ),
        out_specs=(
            P("dp", "row", "col", None),
            P("dp", "row", "col", None),
            P(None, "dp", None),
            P(None, None, "dp"),
            P(),
            P(),
            P(),
        ),
        check_vma=False,
    )
```

profile of v0, /device:TPU:1, one launch (start us, length us, event | category | flops | bytes accessed | tf_op | source)
XLA Modules:
  0.0 646.8 jit_solution(13903822285871508626)
XLA Ops:
  15.0 4.6 collective-permute-start
  33.0 4.2 collective-permute-start.2
  38.8 11.4 %fusion.385 = (f32[16,32]{1,0:T(8,128)S(1)}, f32[1,16,32,512]{3,2,1,0:T(8,128)S(1)}) fusion(f32[512]{0:T(512)S(1)} %bitcast.634, f32[512]{0:T(512)S(1)} %bitcast.461, bf16[1,22,3,512]{3,2,1,0:T(4,128)(2,1)S(1)} %collective-permute-done.3, bf16[1,22,32,512]{3,2,1,0:T(8,128)(2,1)S(1)} %get-tuple-element.312, f32[512]{0:T(512)S(1)} %bitcast.463, ...), kind=kLoop, calls=%fused_computation.850 | loop fusion | flops 71826944 | bytes 5679104 | tf_op jit(solution)/shard_map/reduce_sum | solution.py:122
  52.8 24.5 %all-gather.3.cloned.1.call-done = bf16[512,4096]{0,1:T(8,128)(2,1)} async-done(((bf16[256,4096]{0,1:T(8,128)(2,1)}), bf16[512,4096]{0,1:T(8,128)(2,1)}) %all-gather.3.cloned.1.call-update) | async-done | bytes 4194320 | tf_op jit(solution)/shard_map/all_gather | solution.py:54
  95.9 4.4 collective-permute-done.7
  101.1 9.2 %fusion.383 = (f32[16,32]{1,0:T(8,128)S(1)}, f32[1,16,32,512]{3,2,1,0:T(8,128)}) fusion(f32[512]{0:T(512)S(1)} %bitcast.650, f32[512]{0:T(512)S(1)} %bitcast.529, bf16[1,22,35,512]{3,2,1,0:T(8,128)(2,1)S(1)} %get-tuple-element.193, f32[512]{0:T(512)S(1)} %bitcast.531, f32[512]{0:T(512)S(1)} %bitcast.533, f32[512]{0:T(512)S(1)} %bitcast.536, ...), kind=kLoop, calls=%fused_computation.849 | loop fusion | flops 40369664 | bytes 23894016 | tf_op jit(solution)/shard_map/reduce_sum | solution.py:122
  114.5 24.6 %all-gather.5.cloned.1.call-done = bf16[512,4096]{0,1:T(8,128)(2,1)} async-done(((bf16[256,4096]{0,1:T(8,128)(2,1)}), bf16[512,4096]{0,1:T(8,128)(2,1)}) %all-gather.5.cloned.1.call-update) | async-done | bytes 4194320 | tf_op jit(solution)/shard_map/all_gather | solution.py:54
  142.4 4.2 fusion.406
  162.1 4.6 collective-permute-start.10
  169.4 5.3 all-to-all-start.3
  176.3 10.3 %multiply_reduce_fusion.2 = (f32[512]{0:T(512)}, f32[512]{0:T(512)}, f32[1,16,32,512]{3,2,1,0:T(8,128)S(1)}) fusion(bf16[1,16,32,512]{3,2,1,0:T(8,128)(2,1)} %param.12, f32[512]{0:T(512)} %bitcast.647, f32[512]{0:T(512)} %bitcast.629, f32[512]{0:T(512)S(1)} %bitcast.528, f32[1,22,38,512]{3,2,1,0:T(8,128)S(1)} %maximum_convert_fusion.2, f32[512]{0:T(512)} %bitcast.566, ...), kind=kLoop, calls=%fused_computation.682 | loop fusion | flops 26999808 | bytes 53061632 | tf_op jit(solution)/shard_map/reduce_sum | solution.py:140
  187.6 3.5 multiply_reduce_fusion.1
  191.1 8.7 %all-to-all-done.3 = bf16[2,256,2048]{2,1,0:T(8,128)(2,1)} async-done(((bf16[2,256,2048]{2,1,0:T(8,128)(2,1)}), bf16[2,256,2048]{2,1,0:T(8,128)(2,1)}, u32[]{:S(2)}, u32[]{:S(2)}) %all-to-all-start.3) | async-done | bytes 2097184 | tf_op jit(solution)/shard_map/all_to_all | solution.py:18
  199.8 4.9 all-to-all-start.9
  204.7 6.9 %fusion.407 = (f32[2048]{0:T(1024)}, bf16[512,2048]{1,0:T(8,128)(2,1)S(1)}) fusion(f32[512,2048]{1,0:T(8,128)} %copy-done.9, f32[2048]{0:T(1024)S(1)} %bitcast.707, bf16[512,512]{1,0:T(8,128)(2,1)} %get-tuple-element.186, bf16[512,4096]{0,1:T(8,128)(2,1)} %all-gather.3.cloned.1.call-done), kind=kOutput, calls=%fused_computation.871 | convolution fusion | flops 1095759872 | bytes 8929280 | tf_op jit(solution)/shard_map/dot_general | solution.py:145
  215.5 13.3 %all-to-all-done.9 = bf16[2,2048,256]{1,2,0:T(8,128)(2,1)} async-done(((bf16[2,2048,256]{1,2,0:T(8,128)(2,1)}), bf16[2,2048,256]{1,2,0:T(8,128)(2,1)}, u32[]{:S(2)}, u32[]{:S(2)}) %all-to-all-start.9) | async-done | bytes 2097184 | tf_op jit(solution)/shard_map/all_to_all | solution.py:18
  228.8 5.0 all-to-all-start
  233.9 3.8 fusion.221
  237.7 3.4 convolution_convert_fusion.1
  241.0 16.1 %all-to-all-done = bf16[2,256,2048]{2,1,0:T(8,128)(2,1)} async-done(((bf16[2,256,2048]{2,1,0:T(8,128)(2,1)}), bf16[2,256,2048]{2,1,0:T(8,128)(2,1)}, u32[]{:S(2)}, u32[]{:S(2)}) %all-to-all-start) | async-done | bytes 2097184 | tf_op jit(solution)/shard_map/all_to_all | solution.py:18
  257.2 4.8 all-to-all-start.6
  262.0 3.5 fusion.222
  265.5 3.9 fusion.225
  276.6 7.9 %all-to-all-done.6 = bf16[2,2048,256]{1,2,0:T(8,128)(2,1)} async-done(((bf16[2,2048,256]{1,2,0:T(8,128)(2,1)}), bf16[2,2048,256]{1,2,0:T(8,128)(2,1)}, u32[]{:S(2)}, u32[]{:S(2)}) %all-to-all-start.6) | async-done | bytes 2097184 | tf_op jit(solution)/shard_map/all_to_all | solution.py:18
  284.4 12.6 %all-to-all-start.4 = ((bf16[64,4,2048]{2,1,0:T(4,128)(2,1)}), bf16[64,4,2048]{2,1,0:T(4,128)(2,1)S(1)}, u32[]{:S(2)}, u32[]{:S(2)}) async-start(bf16[64,4,2048]{2,1,0:T(4,128)(2,1)} %reshape.942), calls=%async_computation.4 | async-start | bytes 2097152 | tf_op jit(solution)/shard_map/all_to_all | solution.py:18
  306.4 9.8 %all-to-all-done.4 = bf16[64,4,2048]{2,1,0:T(4,128)(2,1)S(1)} async-done(((bf16[64,4,2048]{2,1,0:T(4,128)(2,1)}), bf16[64,4,2048]{2,1,0:T(4,128)(2,1)S(1)}, u32[]{:S(2)}, u32[]{:S(2)}) %all-to-all-start.4) | async-done | bytes 1048608 | tf_op jit(solution)/shard_map/all_to_all | solution.py:18
  317.2 5.4 all-to-all-start.10
  323.4 5.2 multiply_reduce_fusion.3
  334.1 7.6 %all-to-all-done.10 = bf16[64,32,256]{2,1,0:T(8,128)(2,1)S(1)} async-done(((bf16[64,32,256]{2,1,0:T(8,128)(2,1)}), bf16[64,32,256]{2,1,0:T(8,128)(2,1)S(1)}, u32[]{:S(2)}, u32[]{:S(2)}) %all-to-all-start.10) | async-done | bytes 1048608 | tf_op jit(solution)/shard_map/all_to_all | solution.py:18
  341.7 5.8 all-to-all-start.1
  355.9 3.9 fusion.123
  366.6 9.8 %all-to-all-start.7 = ((bf16[64,32,256]{2,1,0:T(8,128)(2,1)}), bf16[64,32,256]{2,1,0:T(8,128)(2,1)}, u32[]{:S(2)}, u32[]{:S(2)}) async-start(bf16[64,32,256]{2,1,0:T(8,128)(2,1)} %bitcast.446), calls=%async_computation.7 | async-start | bytes 2097152 | tf_op jit(solution)/shard_map/all_to_all | solution.py:18
  376.5 3.5 fusion.125
  380.0 3.9 fusion.127
  387.6 7.8 %all-to-all-done.7 = bf16[64,32,256]{2,1,0:T(8,128)(2,1)} async-done(((bf16[64,32,256]{2,1,0:T(8,128)(2,1)}), bf16[64,32,256]{2,1,0:T(8,128)(2,1)}, u32[]{:S(2)}, u32[]{:S(2)}) %all-to-all-start.7) | async-done | bytes 1048608 | tf_op jit(solution)/shard_map/all_to_all | solution.py:18
  397.0 5.4 all-to-all-start.5
  402.4 4.0 fusion.122
  413.9 7.5 %all-to-all-done.5 = bf16[64,4,2048]{2,1,0:T(4,128)(2,1)S(1)} async-done(((bf16[64,4,2048]{2,1,0:T(4,128)(2,1)}), bf16[64,4,2048]{2,1,0:T(4,128)(2,1)S(1)}, u32[]{:S(2)}, u32[]{:S(2)}) %all-to-all-start.5) | async-done | bytes 1048608 | tf_op jit(solution)/shard_map/all_to_all | solution.py:29
  422.6 5.1 all-to-all-start.11
  429.5 17.4 %all-to-all-done.11 = bf16[64,32,256]{2,1,0:T(8,128)(2,1)S(1)} async-done(((bf16[64,32,256]{2,1,0:T(8,128)(2,1)}), bf16[64,32,256]{2,1,0:T(8,128)(2,1)S(1)}, u32[]{:S(2)}, u32[]{:S(2)}) %all-to-all-start.11) | async-done | bytes 1048608 | tf_op jit(solution)/shard_map/all_to_all | solution.py:29
  448.4 5.9 all-to-all-start.2
  455.2 70.8 %all-reduce = (f32[1,5,512]{2,1,0:T(8,128)S(1)}, f32[1,5,512]{2,1,0:T(8,128)S(1)}, f32[1,2048]{1,0:T(1,128)S(1)}, f32[1,2048]{1,0:T(1,128)S(1)}) all-reduce(f32[1,5,512]{2,1,0:T(8,128)S(1)} %bitcast.457, f32[1,5,512]{2,1,0:T(8,128)S(1)} %bitcast.458, ...), channel_id=1, replica_groups=mesh['row'=16,'col'=4,'dp'=2] {'row','col','dp'}, use_global_device_ids=true, to_apply=%region_127.128 | all-reduce | flops 9216 | bytes 73728 | tf_op jit(solution)/shard_map/psum | solution.py:239
  529.8 4.0 collective-permute-start.14
  533.8 70.9 %all-reduce.4.cloned.1.call-done = (f32[1,7,7,512]{3,2,1,0:T(8,128)}, f32[1,7,7,512]{3,2,1,0:T(8,128)}) async-done(((f32[1,7,7,512]{3,2,1,0:T(8,128)}, f32[1,7,7,512]{3,2,1,0:T(8,128)}), (f32[1,7,7,512]{3,2,1,0:T(8,128)}, f32[1,7,7,512]{3,2,1,0:T(8,128)})) %all-reduce.4.cloned.1.call-update) | async-done | bytes 200720 | tf_op jit(solution)/shard_map/psum | solution.py:239
  610.4 7.1 %all-to-all-start.8 = ((bf16[64,32,256]{2,1,0:T(8,128)(2,1)}), bf16[64,32,256]{2,1,0:T(8,128)(2,1)}, u32[]{:S(2)}, u32[]{:S(2)}) async-start(bf16[64,32,256]{2,1,0:T(8,128)(2,1)} %broadcast_in_dim.10), calls=%async_computation.8 | async-start | bytes 2097152 | tf_op jit(solution)/shard_map/all_to_all | solution.py:29
  617.8 9.0 %fusion.228 = bf16[1,16,32,512]{3,2,1,0:T(8,128)(2,1)} fusion(f32[1,22,38,512]{3,2,1,0:T(8,128)S(1)} %maximum_convert_fusion.3, f32[1,16,32,512]{3,2,1,0:T(8,128)} %copy-done.21, bf16[1,16,32,512]{3,2,1,0:T(8,128)(2,1)S(1)} %copy-done.20, f32[512]{0:T(512)S(1)} %bitcast.462, f32[512]{0:T(512)S(1)} %bitcast.464, f32[512]{0:T(512)S(1)} %bitcast.466, ...), kind=kLoop, calls=%fused_computation.473 | loop fusion | flops 26476544 | bytes 53577728 | tf_op jit(solution)/shard_map/convert_element_type | solution.py:242
  631.9 4.4 all-to-all-done.8
  636.3 3.5 maximum_convert_fusion.1
  (563 shorter events, 146.0 us)
Async XLA Ops:
  7.2 70.1 %all-gather.3.cloned.1.call-start = ((), (), s32[]{:S(2)}) async-start(), calls=%async_computation.12 | async-start | bytes 6291456 | tf_op jit(solution)/shard_map/all_gather | solution.py:54
  14.9 124.2 %all-gather.5.cloned.1.call-start = ((), (), s32[]{:S(2)}) async-start(), calls=%async_computation.13 | async-start | bytes 6291456 | tf_op jit(solution)/shard_map/all_gather | solution.py:54
  15.0 16.4 %collective-permute-start = (bf16[1,3,32,512]{3,2,1,0:T(8,128)(2,1)S(1)}, bf16[1,3,32,512]{3,2,1,0:T(8,128)(2,1)S(1)}, u32[]{:S(2)}, u32[]{:S(2)}) collective-permute-start(bf16[1,3,32,512]{3,2,1,0:T(8,128)(2,1)S(1)} %get-tuple-element.208), channel_id=1, source_target_pairs={{0,8},{8,16},{16,24},{24,32},{32,40},{40,48},{48,56},{56,64},{64,7... | collective-permute-start | bytes 294920 | tf_op jit(solution)/shard_map/ppermute | solution.py:69
  19.6 12.1 %collective-permute-start.1 = (bf16[1,3,32,512]{3,2,1,0:T(8,128)(2,1)S(1)}, bf16[1,3,32,512]{3,2,1,0:T(8,128)(2,1)S(1)}, u32[]{:S(2)}, u32[]{:S(2)}) collective-permute-start(bf16[1,3,32,512]{3,2,1,0:T(8,128)(2,1)S(1)} %get-tuple-element.207), channel_id=1, source_target_pairs={{8,0},{16,8},{24,16},{32,24},{40,32},{48,40},{56,48},{64,56},{72,6... | collective-permute-start | bytes 294920 | tf_op jit(solution)/shard_map/ppermute | solution.py:72
  31.7 6.1 collective-permute-start.3
  33.0 5.7 collective-permute-start.2
  83.4 6.3 collective-permute-start.5
  86.3 4.6 collective-permute-start.4
  91.0 4.8 collective-permute-start.6
  94.2 6.1 collective-permute-start.7
  150.9 9.3 %collective-permute-start.9 = (bf16[1,3,32,512]{3,2,1,0:T(8,128)(2,1)S(1)}, bf16[1,3,32,512]{3,2,1,0:T(8,128)(2,1)S(1)}, u32[]{:S(2)}, u32[]{:S(2)}) collective-permute-start(bf16[1,3,32,512]{3,2,1,0:T(8,128)(2,1)S(1)} %get-tuple-element.201), channel_id=1, source_target_pairs={{8,0},{16,8},{24,16},{32,24},{40,32},{48,40},{56,48},{64,56},{72,6... | collective-permute-start | bytes 294920 | tf_op jit(solution)/shard_map/ppermute | solution.py:72
  153.6 6.5 %collective-permute-start.8 = (bf16[1,3,32,512]{3,2,1,0:T(8,128)(2,1)S(1)}, bf16[1,3,32,512]{3,2,1,0:T(8,128)(2,1)S(1)}, u32[]{:S(2)}, u32[]{:S(2)}) collective-permute-start(bf16[1,3,32,512]{3,2,1,0:T(8,128)(2,1)S(1)} %get-tuple-element.200), channel_id=1, source_target_pairs={{0,8},{8,16},{16,24},{24,32},{32,40},{40,48},{48,56},{56,64},{64,7... | collective-permute-start | bytes 294920 | tf_op jit(solution)/shard_map/ppermute | solution.py:69
  160.9 13.9 %collective-permute-start.11 = (bf16[1,22,3,512]{3,2,1,0:T(4,128)(2,1)}, bf16[1,22,3,512]{3,2,1,0:T(4,128)(2,1)}, u32[]{:S(2)}, u32[]{:S(2)}) collective-permute-start(bf16[1,22,3,512]{3,2,1,0:T(4,128)(2,1)} %get-tuple-element.191), channel_id=1, source_target_pairs={{2,0},{4,2},{6,4},{3,1},{5,3},{7,5},{10,8},{12,10},{14,12},{11,9},... | collective-permute-start | bytes 202760 | tf_op jit(solution)/shard_map/ppermute | solution.py:72
  162.1 12.6 %collective-permute-start.10 = (bf16[1,22,3,512]{3,2,1,0:T(4,128)(2,1)}, bf16[1,22,3,512]{3,2,1,0:T(4,128)(2,1)}, u32[]{:S(2)}, u32[]{:S(2)}) collective-permute-start(bf16[1,22,3,512]{3,2,1,0:T(4,128)(2,1)} %get-tuple-element.190), channel_id=1, source_target_pairs={{0,2},{2,4},{4,6},{1,3},{3,5},{5,7},{8,10},{10,12},{12,14},{9,11},... | collective-permute-start | bytes 202760 | tf_op jit(solution)/shard_map/ppermute | solution.py:69
  169.4 30.3 %all-to-all-start.3 = ((bf16[2,256,2048]{2,1,0:T(8,128)(2,1)}), bf16[2,256,2048]{2,1,0:T(8,128)(2,1)}, u32[]{:S(2)}, u32[]{:S(2)}) async-start(bf16[2,256,2048]{2,1,0:T(8,128)(2,1)} %bitcast.453), calls=%async_computation.3 | async-start | bytes 4194304 | tf_op jit(solution)/shard_map/all_to_all | solution.py:18
  199.8 29.1 %all-to-all-start.9 = ((bf16[2,2048,256]{1,2,0:T(8,128)(2,1)}), bf16[2,2048,256]{1,2,0:T(8,128)(2,1)}, u32[]{:S(2)}, u32[]{:S(2)}) async-start(bf16[2,2048,256]{1,2,0:T(8,128)(2,1)} %bitcast.451), calls=%async_computation.9 | async-start | bytes 4194304 | tf_op jit(solution)/shard_map/all_to_all | solution.py:18
  228.8 28.3 %all-to-all-start = ((bf16[2,256,2048]{2,1,0:T(8,128)(2,1)}), bf16[2,256,2048]{2,1,0:T(8,128)(2,1)}, u32[]{:S(2)}, u32[]{:S(2)}) async-start(bf16[2,256,2048]{2,1,0:T(8,128)(2,1)} %bitcast.454), calls=%async_computation | async-start | bytes 4194304 | tf_op jit(solution)/shard_map/all_to_all | solution.py:18
  257.2 27.3 %all-to-all-start.6 = ((bf16[2,2048,256]{1,2,0:T(8,128)(2,1)}), bf16[2,2048,256]{1,2,0:T(8,128)(2,1)}, u32[]{:S(2)}, u32[]{:S(2)}) async-start(bf16[2,2048,256]{1,2,0:T(8,128)(2,1)} %bitcast.452), calls=%async_computation.6 | async-start | bytes 4194304 | tf_op jit(solution)/shard_map/all_to_all | solution.py:18
  284.4 31.7 %all-to-all-start.4 = ((bf16[64,4,2048]{2,1,0:T(4,128)(2,1)}), bf16[64,4,2048]{2,1,0:T(4,128)(2,1)S(1)}, u32[]{:S(2)}, u32[]{:S(2)}) async-start(bf16[64,4,2048]{2,1,0:T(4,128)(2,1)} %reshape.942), calls=%async_computation.4 | async-start | bytes 2097152 | tf_op jit(solution)/shard_map/all_to_all | solution.py:18
  317.2 24.4 %all-to-all-start.10 = ((bf16[64,32,256]{2,1,0:T(8,128)(2,1)}), bf16[64,32,256]{2,1,0:T(8,128)(2,1)S(1)}, u32[]{:S(2)}, u32[]{:S(2)}) async-start(bf16[64,32,256]{2,1,0:T(8,128)(2,1)} %bitcast.447), calls=%async_computation.10 | async-start | bytes 2097152 | tf_op jit(solution)/shard_map/all_to_all | solution.py:18
  341.7 24.9 %all-to-all-start.1 = ((bf16[64,4,2048]{2,1,0:T(4,128)(2,1)}), bf16[64,4,2048]{2,1,0:T(4,128)(2,1)}, u32[]{:S(2)}, u32[]{:S(2)}) async-start(bf16[64,4,2048]{2,1,0:T(4,128)(2,1)} %reshape.940), calls=%async_computation.1 | async-start | bytes 2097152 | tf_op jit(solution)/shard_map/all_to_all | solution.py:18
  350.1 177.5 %collective-permute-start.13 = (bf16[1,3,32,512]{3,2,1,0:T(8,128)(2,1)}, bf16[1,3,32,512]{3,2,1,0:T(8,128)(2,1)}, u32[]{:S(2)}, u32[]{:S(2)}) collective-permute-start(bf16[1,3,32,512]{3,2,1,0:T(8,128)(2,1)} %get-tuple-element.199), channel_id=1, source_target_pairs={{8,0},{16,8},{24,16},{32,24},{40,32},{48,40},{56,48},{64,56},{72,6... | collective-permute-start | bytes 294920 | tf_op jit(solution)/shard_map/ppermute | solution.py:72
  352.7 174.9 %collective-permute-start.12 = (bf16[1,3,32,512]{3,2,1,0:T(8,128)(2,1)}, bf16[1,3,32,512]{3,2,1,0:T(8,128)(2,1)}, u32[]{:S(2)}, u32[]{:S(2)}) collective-permute-start(bf16[1,3,32,512]{3,2,1,0:T(8,128)(2,1)} %get-tuple-element.198), channel_id=1, source_target_pairs={{0,8},{8,16},{16,24},{24,32},{32,40},{40,48},{48,56},{56,64},{64,7... | collective-permute-start | bytes 294920 | tf_op jit(solution)/shard_map/ppermute | solution.py:69
  366.6 28.8 %all-to-all-start.7 = ((bf16[64,32,256]{2,1,0:T(8,128)(2,1)}), bf16[64,32,256]{2,1,0:T(8,128)(2,1)}, u32[]{:S(2)}, u32[]{:S(2)}) async-start(bf16[64,32,256]{2,1,0:T(8,128)(2,1)} %bitcast.446), calls=%async_computation.7 | async-start | bytes 2097152 | tf_op jit(solution)/shard_map/all_to_all | solution.py:18
  397.0 24.5 %all-to-all-start.5 = ((bf16[64,4,2048]{2,1,0:T(4,128)(2,1)}), bf16[64,4,2048]{2,1,0:T(4,128)(2,1)S(1)}, u32[]{:S(2)}, u32[]{:S(2)}) async-start(bf16[64,4,2048]{2,1,0:T(4,128)(2,1)} %broadcast_in_dim.9), calls=%async_computation.5 | async-start | bytes 2097152 | tf_op jit(solution)/shard_map/all_to_all | solution.py:29
  413.9 113.7 %copy-start.16 = (bf16[1,16,32,512]{3,2,1,0:T(8,128)(2,1)S(1)}, bf16[1,16,32,512]{3,2,1,0:T(8,128)(2,1)}, u32[]{:S(2)}) copy-start(bf16[1,16,32,512]{3,2,1,0:T(8,128)(2,1)} %copy-done.15) | copy-start | bytes 1572868
  421.4 105.2 %copy-start.22 = (bf16[64,4,2048]{2,1,0:T(4,128)(2,1)}, bf16[64,4,2048]{2,1,0:T(4,128)(2,1)S(1)}, u32[]{:S(2)}) copy-start(bf16[64,4,2048]{2,1,0:T(4,128)(2,1)S(1)} %all-to-all-done.5) | copy-start | bytes 3145732
  422.6 24.2 %all-to-all-start.11 = ((bf16[64,32,256]{2,1,0:T(8,128)(2,1)}), bf16[64,32,256]{2,1,0:T(8,128)(2,1)S(1)}, u32[]{:S(2)}, u32[]{:S(2)}) async-start(bf16[64,32,256]{2,1,0:T(8,128)(2,1)} %broadcast_in_dim.11), calls=%async_computation.11 | async-start | bytes 2097152 | tf_op jit(solution)/shard_map/all_to_all | solution.py:29
  446.9 159.7 %copy-start.25 = (bf16[64,32,256]{2,1,0:T(8,128)(2,1)}, bf16[64,32,256]{2,1,0:T(8,128)(2,1)S(1)}, u32[]{:S(2)}) copy-start(bf16[64,32,256]{2,1,0:T(8,128)(2,1)S(1)} %all-to-all-done.11) | copy-start | bytes 3145732
  448.4 160.9 %all-to-all-start.2 = ((bf16[64,4,2048]{2,1,0:T(4,128)(2,1)}), bf16[64,4,2048]{2,1,0:T(4,128)(2,1)}, u32[]{:S(2)}, u32[]{:S(2)}) async-start(bf16[64,4,2048]{2,1,0:T(4,128)(2,1)} %broadcast_in_dim.8), calls=%async_computation.2 | async-start | bytes 2097152 | tf_op jit(solution)/shard_map/all_to_all | solution.py:29
  454.2 150.5 %all-reduce.4.cloned.1.call-start = ((), (), s32[]{:S(2)}) async-start(), calls=%async_computation.14 | async-start | bytes 458752 | tf_op jit(solution)/shard_map/psum | solution.py:239
  527.3 90.2 %copy-start.50 = (f32[1,1,512]{2,1,0:T(1,128)S(1)}, f32[1,1,512]{2,1,0:T(1,128)}, u32[]{:S(2)}) copy-start(f32[1,1,512]{2,1,0:T(1,128)} %copy-done.49) | copy-start | bytes 6148
  527.3 90.2 %copy-start.52 = (f32[1,1,512]{2,1,0:T(1,128)S(1)}, f32[1,1,512]{2,1,0:T(1,128)}, u32[]{:S(2)}) copy-start(f32[1,1,512]{2,1,0:T(1,128)} %copy-done.51) | copy-start | bytes 6148
  527.3 90.2 %copy-start.54 = (f32[1,1,512]{2,1,0:T(1,128)S(1)}, f32[1,1,512]{2,1,0:T(1,128)}, u32[]{:S(2)}) copy-start(f32[1,1,512]{2,1,0:T(1,128)} %copy-done.53) | copy-start | bytes 6148
  527.3 90.2 %copy-start.56 = (f32[1,1,512]{2,1,0:T(1,128)S(1)}, f32[1,1,512]{2,1,0:T(1,128)}, u32[]{:S(2)}) copy-start(f32[1,1,512]{2,1,0:T(1,128)} %copy-done.55) | copy-start | bytes 6148
  527.3 90.2 %copy-start.58 = (f32[1,1,512]{2,1,0:T(1,128)S(1)}, f32[1,1,512]{2,1,0:T(1,128)}, u32[]{:S(2)}) copy-start(f32[1,1,512]{2,1,0:T(1,128)} %copy-done.57) | copy-start | bytes 6148
  527.3 90.2 %copy-start.60 = (f32[1,1,512]{2,1,0:T(1,128)S(1)}, f32[1,1,512]{2,1,0:T(1,128)}, u32[]{:S(2)}) copy-start(f32[1,1,512]{2,1,0:T(1,128)} %copy-done.59) | copy-start | bytes 6148
  527.4 90.2 %copy-start.62 = (f32[1,1,512]{2,1,0:T(1,128)S(1)}, f32[1,1,512]{2,1,0:T(1,128)}, u32[]{:S(2)}) copy-start(f32[1,1,512]{2,1,0:T(1,128)} %copy-done.61) | copy-start | bytes 6148
  527.4 90.2 %copy-start.64 = (f32[1,1,512]{2,1,0:T(1,128)S(1)}, f32[1,1,512]{2,1,0:T(1,128)}, u32[]{:S(2)}) copy-start(f32[1,1,512]{2,1,0:T(1,128)} %copy-done.63) | copy-start | bytes 6148
  527.4 90.2 %copy-start.66 = (f32[1,1,512]{2,1,0:T(1,128)S(1)}, f32[1,1,512]{2,1,0:T(1,128)}, u32[]{:S(2)}) copy-start(f32[1,1,512]{2,1,0:T(1,128)} %copy-done.65) | copy-start | bytes 6148
  527.4 90.2 %copy-start.68 = (f32[1,1,512]{2,1,0:T(1,128)S(1)}, f32[1,1,512]{2,1,0:T(1,128)}, u32[]{:S(2)}) copy-start(f32[1,1,512]{2,1,0:T(1,128)} %copy-done.67) | copy-start | bytes 6148
  527.4 90.2 %copy-start.70 = (f32[1,1,512]{2,1,0:T(1,128)S(1)}, f32[1,1,512]{2,1,0:T(1,128)}, u32[]{:S(2)}) copy-start(f32[1,1,512]{2,1,0:T(1,128)} %copy-done.69) | copy-start | bytes 6148
  527.4 90.2 %copy-start.72 = (f32[1,1,512]{2,1,0:T(1,128)S(1)}, f32[1,1,512]{2,1,0:T(1,128)}, u32[]{:S(2)}) copy-start(f32[1,1,512]{2,1,0:T(1,128)} %copy-done.71) | copy-start | bytes 6148
  527.4 90.2 %copy-start.74 = (f32[1,1,512]{2,1,0:T(1,128)S(1)}, f32[1,1,512]{2,1,0:T(1,128)}, u32[]{:S(2)}) copy-start(f32[1,1,512]{2,1,0:T(1,128)} %copy-done.73) | copy-start | bytes 6148
  527.4 90.2 %copy-start.76 = (f32[1,1,512]{2,1,0:T(1,128)S(1)}, f32[1,1,512]{2,1,0:T(1,128)}, u32[]{:S(2)}) copy-start(f32[1,1,512]{2,1,0:T(1,128)} %copy-done.75) | copy-start | bytes 6148
  528.5 78.1 %collective-permute-start.15 = (bf16[1,22,3,512]{3,2,1,0:T(4,128)(2,1)S(1)}, bf16[1,22,3,512]{3,2,1,0:T(4,128)(2,1)S(1)}, u32[]{:S(2)}, u32[]{:S(2)}) collective-permute-start(bf16[1,22,3,512]{3,2,1,0:T(4,128)(2,1)S(1)} %get-tuple-element.189), channel_id=1, source_target_pairs={{2,0},{4,2},{6,4},{3,1},{5,3},{7,5},{10,8},{12,10},{14,12},{11,9},... | collective-permute-start | bytes 202760 | tf_op jit(solution)/shard_map/ppermute | solution.py:72
  529.8 76.8 %collective-permute-start.14 = (bf16[1,22,3,512]{3,2,1,0:T(4,128)(2,1)S(1)}, bf16[1,22,3,512]{3,2,1,0:T(4,128)(2,1)S(1)}, u32[]{:S(2)}, u32[]{:S(2)}) collective-permute-start(bf16[1,22,3,512]{3,2,1,0:T(4,128)(2,1)S(1)} %get-tuple-element.188), channel_id=1, source_target_pairs={{0,2},{2,4},{4,6},{1,3},{3,5},{5,7},{8,10},{10,12},{12,14},{9,11},... | collective-permute-start | bytes 202760 | tf_op jit(solution)/shard_map/ppermute | solution.py:69
  610.4 25.9 %all-to-all-start.8 = ((bf16[64,32,256]{2,1,0:T(8,128)(2,1)}), bf16[64,32,256]{2,1,0:T(8,128)(2,1)}, u32[]{:S(2)}, u32[]{:S(2)}) async-start(bf16[64,32,256]{2,1,0:T(8,128)(2,1)} %broadcast_in_dim.10), calls=%async_computation.8 | async-start | bytes 2097152 | tf_op jit(solution)/shard_map/all_to_all | solution.py:29
  (188 other events, 5064.3 us)
Sparse Core Ops, SparseCore 0:
  15.0 62.2 all-gather.2
  78.9 60.1 all-gather.4
  460.6 144.1 all-reduce.3
where the time goes:
time: 657 us; the launch traced here: 647 us
  waiting for transfers between devices  229 us (35%)
  starting transfers between devices  123 us (19%)
  other arithmetic  115 us (18%)
  blocking collectives  70.8 us (11%)
  local copies, waits for them, and re-layouts  49.2 us (7%)
  matrix products  42.8 us (7%)
  between operations  17.6 us (3%)
    all_to_all x8, waiting for transfers between devices, sent_and_summed(): pieces = lax.all_to_all(cut_along(shard, dim, size), axis, 0, 0, tiled=True)  72.5 us
    psum x1, waiting for transfers between devices, per_device(): lax.psum((local_taps, channel_grads, grad_bias), ('row', 'col', 'dp'))  70.9 us
    psum x1, blocking collectives, per_device(): lax.psum((local_taps, channel_grads, grad_bias), ('row', 'col', 'dp'))  70.8 us
    all_to_all x8, starting transfers between devices, sent_and_summed(): pieces = lax.all_to_all(cut_along(shard, dim, size), axis, 0, 0, tiled=True)  53.7 us
    all_gather x2, waiting for transfers between devices, turned_gather(): result = lax.all_gather(both, axis, axis=0, tiled=True)  49.1 us
    ppermute x8, starting transfers between devices, with_halo(): lax.ppermute(lax.slice_in_dim(block, block.shape[dim] - width, None, axis...  29.9 us
    all_to_all x4, waiting for transfers between devices, copy_for_each(): return lax.all_to_all(copies, axis, split_axis=0, concat_axis=0, tiled=True)  29.4 us
    reduce_sum x9, other arithmetic, tap_grads(): line.append(jnp.sum(window * upstream, axis=(0, 1, 2)))  29.3 us
  transfers between devices with their start and end apart: 31, of which 18 were waited for; matrix products, arithmetic and copies ran while one was open for 27% of the time, Pallas kernels for 0%

commit v1 on v0

--- a/solution.py
+++ b/solution.py
@@ -8,57 +8,46 @@
 EPSILON = 1e-06
 
 
-def cut_along(shard, dim, size):
-    before, after = (shard.shape[:dim], shard.shape[dim + 1 :])
-    return jnp.moveaxis(shard.reshape(*before, size, -1, *after), dim, 0)
-
-
-def sent_and_summed(shard, axis, dim):
-    size = lax.axis_size(axis)
-    pieces = lax.all_to_all(cut_along(shard, dim, size), axis, 0, 0, tiled=True)
-    return jnp.sum(pieces.astype(jnp.float32), axis=0)
-
-
-def padded_to(lines, size):
-    spare = -len(lines) % size
-    return jnp.pad(lines, [(0, spare)] + [(0, 0)] * (lines.ndim - 1))
-
-
-def copy_for_each(shard, axis):
-    copies = jnp.broadcast_to(shard, (lax.axis_size(axis), *shard.shape))
-    return lax.all_to_all(copies, axis, split_axis=0, concat_axis=0, tiled=True)
-
-
-def in_order(pieces, dim):
-    pieces = jnp.moveaxis(pieces, 0, dim)
-    lengths = pieces.shape
-    return pieces.reshape(*lengths[:dim], lengths[dim] * lengths[dim + 1], *lengths[dim + 2 :])
-
-
-def gather_directly(shard, axis, dim):
-    pieces = copy_for_each(shard, axis)
-    return in_order(pieces, dim)
-
-
-def total_of(shard, axes):
-    lines = shard.reshape(-1, shard.shape[-1])
-    padded = padded_to(lines, lax.axis_size(axes))
-    whole = gather_directly(sent_and_summed(padded, axes, 0).astype(jnp.bfloat16), axes, 0)
-    return lax.slice_in_dim(whole, 0, len(lines)).reshape(shard.shape).astype(jnp.float32)
-
-
-def turned_gather(arrays, axis, dims):
-    turned = [jnp.moveaxis(a, dim, 0) for a, dim in zip(arrays, dims)]
-    widths = [t[0].size for t in turned]
-    both = jnp.concatenate([t.reshape(-1, w) for t, w in zip(turned, widths)], axis=1)
-    result = lax.all_gather(both, axis, axis=0, tiled=True)
-    pieces = jnp.split(result, [sum(widths[:k]) for k in range(1, len(widths))], axis=1)
-    return tuple(
-        (
-            jnp.moveaxis(b.reshape(-1, *t.shape[1:]), 0, dim)
-            for b, t, dim in zip(pieces, turned, dims)
-        )
-    )
+SPACE = ("xh", "y", "z")
+HALF = 1024
+
+
+def chips_along_x(step):
+    def target(pos):
+        x = (pos + step) % 4
+        return x
+
+    return [(pos, target(pos)) for pos in range(4)]
+
+
+def swapped(value, axis):
+    return lax.ppermute(value, axis, [(0, 1), (1, 0)])
+
+
+def fetch_weights(own_in, own_out):
+    core = lax.axis_index("core")
+    part = lax.axis_index("dp")
+    send_in = lax.dynamic_slice_in_dim(own_in, core * 128, 128, 0)
+    send_out = lax.dynamic_slice_in_dim(own_out, core * 1024, 1024, 0)
+    got_in = lax.ppermute(send_in, ("xh", "dp"), chips_along_x(1))
+    got_out = lax.ppermute(send_out, ("xh", "dp"), chips_along_x(-1))
+    mate_in = swapped(got_in, "core")
+    mate_out = swapped(got_out, "core")
+    first = core == 0
+    other_in = jnp.concatenate(
+        [jnp.where(first, got_in, mate_in), jnp.where(first, mate_in, got_in)], 0
+    )
+    other_out = jnp.concatenate(
+        [jnp.where(first, got_out, mate_out), jnp.where(first, mate_out, got_out)], 0
+    )
+    low = part == 0
+    full_in = jnp.concatenate(
+        [jnp.where(low, own_in, other_in), jnp.where(low, other_in, own_in)], 0
+    )
+    full_out = jnp.concatenate(
+        [jnp.where(low, own_out, other_out), jnp.where(low, other_out, own_out)], 1
+    )
+    return full_in, full_out
 
 
 def with_halo(block, sides, width):
@@ -140,7 +129,7 @@
     grad_bias_out = jnp.sum(grad_branch, 0)
     branch_low = grad_branch.astype(jnp.bfloat16)
     grad_weight_out = lax.dot_general(
-        activated, branch_low, contract_rows, preferred_element_type=jnp.float32
+        branch_low, activated, contract_rows, preferred_element_type=jnp.float32
     )
     grad_act = lax.dot_general(
         branch_low, weight_out, contract_cols, preferred_element_type=jnp.float32
@@ -168,15 +157,39 @@
 
 
 def reduce_weights(grad_in, grad_out):
-    half_in, half_out = (
-        sent_and_summed(grad_in.astype(jnp.bfloat16), "dp", 0),
-        sent_and_summed(grad_out.astype(jnp.bfloat16), "dp", 1),
-    )
-    shard_in, shard_out = (
-        total_of(half_in.astype(jnp.bfloat16), ("row", "col")),
-        total_of(half_out.astype(jnp.bfloat16), ("row", "col")),
-    )
-    return (shard_in, shard_out)
+    core = lax.axis_index("core")
+    both = jnp.stack([grad_in, grad_out], 1).astype(jnp.bfloat16)
+    keep = lax.dynamic_slice_in_dim(both, core * HALF, HALF, 2)
+    give = lax.dynamic_slice_in_dim(both, (1 - core) * HALF, HALF, 2)
+    pair = keep.astype(jnp.float32) + swapped(give, "core").astype(jnp.float32)
+    pair = pair.astype(jnp.bfloat16).reshape(64, 8, 2, HALF)
+    pieces = lax.all_to_all(pair, ("dp", *SPACE), 0, 0, tiled=True)
+    mine = jnp.sum(pieces.astype(jnp.float32), 0).astype(jnp.bfloat16)
+    copies = jnp.broadcast_to(mine, (32, *mine.shape))
+    whole = lax.all_to_all(copies, SPACE, 0, 0, tiled=True).reshape(256, 2, HALF)
+    mate = swapped(whole, "core")
+    first = core == 0
+    full = jnp.concatenate(
+        [jnp.where(first, whole, mate), jnp.where(first, mate, whole)], 2
+    ).astype(jnp.float32)
+    return full[:, 0], full[:, 1].T
+
+
+def reduce_small(parts):
+    axes = ("xh", "y", "core", "z", "dp")
+    lines = jnp.concatenate([p.reshape(-1) for p in parts])
+    count = lines.shape[0]
+    spare = -count % (128 * 128)
+    lines = jnp.pad(lines, (0, spare)).astype(jnp.bfloat16).reshape(128, -1)
+    pieces = lax.all_to_all(lines, axes, 0, 0, tiled=True)
+    mine = jnp.sum(pieces.astype(jnp.float32), 0, keepdims=True)
+    whole = lax.all_gather(mine, axes, axis=0, tiled=True).reshape(-1)
+    outs = []
+    start = 0
+    for p in parts:
+        outs.append(whole[start : start + p.size].reshape(p.shape))
+        start += p.size
+    return outs
 
 
 def per_device(
@@ -199,9 +212,9 @@
     paddings = []
     fetched = []
     for which in range(layers):
-        full_in, full_out = turned_gather((weight_in[which], weight_out[which]), "dp", (0, 1))
+        full_in, full_out = fetch_weights(weight_in[which], weight_out[which])
         fetched.append((full_in, full_out))
-        padded = with_halo(current, (("row", 1), ("col", 2)), 3)
+        padded = with_halo(current, ((("xh", "y", "core"), 1), ("z", 2)), 3)
         current, cache = forward_layer(
             padded,
             current,
@@ -229,35 +242,36 @@
             upstream, caches[which], norm_gain[which], full_in, full_out, layer_scale[which]
         )
         shaped = grad_mixed.reshape(slides.shape)
-        rim = with_halo(shaped.astype(jnp.bfloat16), (("row", 1), ("col", 2)), 3).astype(
+        rim = with_halo(shaped.astype(jnp.bfloat16), ((("xh", "y", "core"), 1), ("z", 2)), 3).astype(
             shaped.dtype
         )
         local_taps = tap_grads(paddings[which], shaped)
         back = depthwise(rim, kernel[which][::-1, ::-1])
         upstream = upstream + back.reshape(-1, channels)
         grads_in[which], grads_out[which] = reduce_weights(grad_in, grad_out)
-        grads_kernel[which], grads_channel[which], grads_bias[which] = lax.psum(
-            (local_taps, channel_grads, grad_bias), ("row", "col", "dp")
+        grads_kernel[which], grads_channel[which], grads_bias[which] = (
+            local_taps,
+            channel_grads,
+            grad_bias,
         )
     grad_slides = upstream.astype(jnp.bfloat16).reshape(slides.shape)
-    return (
-        current,
-        grad_slides,
-        jnp.stack(grads_in),
-        jnp.stack(grads_out),
-        jnp.stack(grads_kernel),
-        jnp.stack(grads_channel),
-        jnp.stack(grads_bias),
-    )
+    small = reduce_small(
+        [jnp.stack(grads_kernel), jnp.stack(grads_channel), jnp.stack(grads_bias)]
+    )
+    return (current, grad_slides, jnp.stack(grads_in), jnp.stack(grads_out), *small)
 
 
 def solution(mesh):
+    fine = jax.sharding.Mesh(
+        mesh.devices.reshape(2, 4, 2, 4, 2), ("xh", "y", "core", "z", "dp")
+    )
+    rows = ("xh", "y", "core")
     return jax.shard_map(
         per_device,
-        mesh=mesh,
+        mesh=fine,
         in_specs=(
-            P("dp", "row", "col", None),
-            P("dp", "row", "col", None),
+            P("dp", rows, "z", None),
+            P("dp", rows, "z", None),
             P(),
             P(),
             P(),
@@ -269,8 +283,8 @@
             P(),
         ),
         out_specs=(
-            P("dp", "row", "col", None),
-            P("dp", "row", "col", None),
+            P("dp", rows, "z", None),
+            P("dp", rows, "z", None),
             P(None, "dp", None),
             P(None, None, "dp"),
             P(),

time: 657 us -> 729 us (1.11)
  blocking collectives: 70.8 us -> 294 us
  waiting for transfers between devices: 229 us -> 76 us
  local copies, waits for them, and re-layouts: 49.2 us -> 85.3 us
  between operations: 17.6 us -> 3.3 us
  matrix products: 42.8 us -> 28.8 us
    all_gather x0 -> x1, blocking collectives: none -> 294 us  [reduce_small(): whole = lax.all_gather(mine, axes, axis=0, tiled=True).reshape(-1)]
    psum x1 -> x0, waiting for transfers between devices: 70.9 us -> none  [per_device(): lax.psum((local_taps, channel_grads, grad_bias), ('row', 'col', 'dp'))]
    psum x1 -> x0, blocking collectives: 70.8 us -> none  [per_device(): lax.psum((local_taps, channel_grads, grad_bias), ('row', 'col', 'dp'))]
    all_gather x2 -> x0, waiting for transfers between devices: 49.1 us -> none  [turned_gather(): result = lax.all_gather(both, axis, axis=0, tiled=True)]
    all_to_all x12 -> x5, waiting for transfers between devices: 102 us -> 64.4 us  [the longest x2 46 us: reduce_weights(): pieces = lax.all_to_all(pair, ('dp', *SPACE), 0, 0, tiled=True)]
    all_to_all x12 -> x5, starting transfers between devices: 77.2 us -> 42.8 us  [the longest x1 14.5 us: reduce_small(): pieces = lax.all_to_all(lines, axes, 0, 0, tiled=True)]
    ppermute x0 -> x12, starting transfers between devices: none -> 26.2 us  [the longest x8 21.5 us: swapped(): return lax.ppermute(value, axis, [(0, 1), (1, 0)])]
    another operation x14 -> x112, local copies, waits for them, and re-layouts: 8.89 us -> 32.1 us  [tap_grads(): rows_out.append(jnp.stack(line))]
  transfers between devices with their start and end apart: 31 -> 33, of which waited for: 18 -> 8; matrix products, arithmetic and copies ran while one was open for 27% -> 22% of each run, Pallas kernels for 0% -> 0%
where the time goes in v1:
time: 729 us; the launch traced here: 721 us
  blocking collectives  294 us (40%)
  starting transfers between devices  117 us (16%)
  other arithmetic  116 us (16%)
  local copies, waits for them, and re-layouts  85.3 us (12%)
  waiting for transfers between devices  76 us (10%)
  matrix products  28.8 us (4%)
    all_gather x1, blocking collectives, reduce_small(): whole = lax.all_gather(mine, axes, axis=0, tiled=True).reshape(-1)  294 us
    all_to_all x2, waiting for transfers between devices, reduce_weights(): pieces = lax.all_to_all(pair, ('dp', *SPACE), 0, 0, tiled=True)  46 us
    ppermute x8, starting transfers between devices, with_halo(): lax.ppermute(lax.slice_in_dim(block, block.shape[dim] - width, None, axis...  32.4 us
    another operation x112, local copies, waits for them, and re-layouts, tap_grads(): rows_out.append(jnp.stack(line))  32.1 us
    reduce_sum x2, other arithmetic, forward_layer(): center = mixed - jnp.mean(mixed, -1, keepdims=True)  27 us
    reduce_sum x9, other arithmetic, tap_grads(): line.append(jnp.sum(window * upstream, axis=(0, 1, 2)))  23.6 us
    ppermute x8, starting transfers between devices, swapped(): return lax.ppermute(value, axis, [(0, 1), (1, 0)])  21.5 us
    ppermute x8, starting transfers between devices, with_halo(): lax.ppermute(lax.slice_in_dim(block, 0, width, axis=dim), axis, backward)  16 us
  transfers between devices with their start and end apart: 33, of which 8 were waited for; matrix products, arithmetic and copies ran while one was open for 22% of the time, Pallas kernels for 0%

profile of v1, /device:TPU:1, one launch (start us, length us, event | category | flops | bytes accessed | tf_op | source)
XLA Modules:
  0.0 720.8 jit_solution(1753578063245275340)
XLA Ops:
  0.6 2.8 fusion.397
  5.4 3.3 collective-permute-start.14
  11.6 4.3 collective-permute-start
  34.6 4.2 collective-permute-start.2
  41.0 15.6 %fusion.394 = (f32[16,32]{1,0:T(8,128)S(1)}, f32[1,16,32,512]{3,2,1,0:T(8,128)S(1)}) fusion(f32[512]{0:T(512)} %bitcast.599, f32[512]{0:T(512)S(1)} %bitcast.396, bf16[1,22,3,512]{3,2,1,0:T(4,128)(2,1)} %copy-done.36, bf16[1,22,32,512]{3,2,1,0:T(8,128)(2,1)S(1)} %get-tuple-element.321, f32[512]{0:T(512)S(1)} %bitcast.398, f32[512]{0:T(512)S(1)} %bitcast.400, ...), kind=kLoop, calls=%fused_computation.914 | loop fusion | flops 71826944 | bytes 5679104 | tf_op jit(solution)/shard_map/reduce_sum | solution.py:111
  56.6 3.1 collective-permute-start.13
  65.3 2.5 bitcast_select_fusion.3
  72.2 2.3 bitcast_select_fusion.1
  74.5 2.6 fusion.327
  77.3 2.3 collective-permute-start.9
  79.6 3.3 collective-permute-start.8
  84.6 3.6 collective-permute-start.10
  90.7 3.0 collective-permute-done.11
  95.5 11.4 %fusion.392 = (f32[16,32]{1,0:T(8,128)S(1)}, f32[1,16,32,512]{3,2,1,0:T(8,128)}) fusion(f32[512]{0:T(512)} %bitcast.604, f32[512]{0:T(512)S(1)} %bitcast.494, bf16[1,22,35,512]{3,2,1,0:T(8,128)(2,1)S(1)} %get-tuple-element.200, f32[512]{0:T(512)S(1)} %bitcast.497, f32[512]{0:T(512)S(1)} %bitcast.499, f32[512]{0:T(512)S(1)} %bitcast.501, ...), kind=kLoop, calls=%fused_computation.913 | loop fusion | flops 40369664 | bytes 23894016 | tf_op jit(solution)/shard_map/reduce_sum | solution.py:111
  110.2 2.8 fusion.24
  113.1 4.2 fusion.416
  122.8 4.3 fusion.223
  127.1 3.4 fusion.219
  133.1 5.6 collective-permute-start.16
  140.3 2.2 fusion.220
  154.4 4.2 collective-permute-start.18
  184.8 10.3 %multiply_reduce_fusion.2 = (bf16[512]{0:T(512)(128)(2,1)}, bf16[512]{0:T(512)(128)(2,1)S(1)}, f32[1,16,32,512]{3,2,1,0:T(8,128)S(1)}) fusion(bf16[1,16,32,512]{3,2,1,0:T(8,128)(2,1)} %param.12, f32[512]{0:T(512)} %bitcast.601, f32[512]{0:T(512)} %bitcast.591, f32[512]{0:T(512)S(1)} %bitcast.493, f32[1,22,38,512]{3,2,1,0:T(8,128)S(1)} %maximum_convert_fusion.2, ...), kind=kLoop, calls=%fused_computation.716 | loop fusion | flops 26999808 | bytes 53059584 | tf_op jit(solution)/shard_map/reduce_sum | solution.py:129
  195.2 3.4 multiply_reduce_fusion.1
  198.8 3.6 fusion.417
  217.8 3.7 fusion.121
  221.6 2.9 fusion.123
  228.7 2.2 fusion.124
  234.5 14.5 %all-to-all-start.4 = ((bf16[128,2,256]{2,1,0:T(2,128)(2,1)}), bf16[128,2,256]{2,1,0:T(2,128)(2,1)S(1)}, u32[]{:S(2)}, u32[]{:S(2)}) async-start(bf16[128,2,256]{2,1,0:T(2,128)(2,1)} %reshape.941), calls=%async_computation.4 | async-start | bytes 262144 | tf_op jit(solution)/shard_map/all_to_all | solution.py:184
  249.1 3.1 fusion.17
  253.8 5.1 all-to-all-done.4
  258.9 5.7 all-to-all-start.2
  264.6 3.1 fusion.16
  269.3 22.3 %all-to-all-done.2 = bf16[64,8,2,1024]{3,1,2,0:T(8,128)(2,1)} async-done(((bf16[64,8,2,1024]{3,1,2,0:T(8,128)(2,1)}), bf16[64,8,2,1024]{3,1,2,0:T(8,128)(2,1)}, u32[]{:S(2)}, u32[]{:S(2)}) %all-to-all-start.2) | async-done | bytes 2097184 | tf_op jit(solution)/shard_map/all_to_all | solution.py:166
  291.7 8.1 %all-to-all-start = ((bf16[64,8,2,1024]{3,1,2,0:T(8,128)(2,1)}), bf16[64,8,2,1024]{3,1,2,0:T(8,128)(2,1)}, u32[]{:S(2)}, u32[]{:S(2)}) async-start(bf16[64,8,2,1024]{3,1,2,0:T(8,128)(2,1)} %copy.26), calls=%async_computation | async-start | bytes 4194304 | tf_op jit(solution)/shard_map/all_to_all | solution.py:166
  301.7 23.7 %all-to-all-done = bf16[64,8,2,1024]{3,1,2,0:T(8,128)(2,1)} async-done(((bf16[64,8,2,1024]{3,1,2,0:T(8,128)(2,1)}), bf16[64,8,2,1024]{3,1,2,0:T(8,128)(2,1)}, u32[]{:S(2)}, u32[]{:S(2)}) %all-to-all-start) | async-done | bytes 2097184 | tf_op jit(solution)/shard_map/all_to_all | solution.py:166
  326.4 8.3 %all-to-all-start.3 = ((bf16[32,8,2,1024]{3,1,2,0:T(8,128)(2,1)}), bf16[32,8,2,1024]{3,1,2,0:T(8,128)(2,1)S(1)}, u32[]{:S(2)}, u32[]{:S(2)}) async-start(bf16[32,8,2,1024]{3,1,2,0:T(8,128)(2,1)} %broadcast_in_dim.7), calls=%async_computation.3 | async-start | bytes 2097152 | tf_op jit(solution)/shard_map/all_to_all | solution.py:169
  337.0 13.3 %all-to-all-done.3 = bf16[32,8,2,1024]{3,1,2,0:T(8,128)(2,1)S(1)} async-done(((bf16[32,8,2,1024]{3,1,2,0:T(8,128)(2,1)}), bf16[32,8,2,1024]{3,1,2,0:T(8,128)(2,1)S(1)}, u32[]{:S(2)}, u32[]{:S(2)}) %all-to-all-start.3) | async-done | bytes 1048608 | tf_op jit(solution)/shard_map/all_to_all | solution.py:169
  351.4 6.2 all-to-all-start.1
  357.6 4.2 collective-permute-start.21
  361.8 3.2 collective-permute-start.20
  365.1 6.7 collective-permute-done.21
  373.2 4.0 collective-permute-start.22
  377.6 293.8 %all-gather.1 = f32[128,1,512]{2,1,0:T(1,128)S(1)} all-gather(f32[1,1,512]{2,1,0:T(1,128)S(1)} %bitcast.600), channel_id=2, replica_groups=mesh['xh'=2,'y'=4,'core'=2,'z'=4,'dp'=2] {'xh','y','core','z','dp'}, dimensions={0}, use_global_device_ids=true | all-gather | bytes 264192 | tf_op jit(solution)/shard_map/all_gather | solution.py:186
  676.6 16.4 %collective-permute-start.27 = (bf16[256,2,1024]{2,0,1:T(8,128)(2,1)}, bf16[256,2,1024]{2,0,1:T(8,128)(2,1)}, u32[]{:S(2)}, u32[]{:S(2)}) collective-permute-start(bf16[256,2,1024]{2,0,1:T(8,128)(2,1)} %bitcast.371), channel_id=1, source_target_pairs={{0,8},{8,0},{1,9},{9,1},{2,10},{10,2},{3,11},{11,3},{4,12},{12,4},... | collective-permute-start | bytes 3145736 | tf_op jit(solution)/shard_map/ppermute | solution.py:24
  694.5 9.4 %fusion.226 = bf16[1,16,32,512]{3,2,1,0:T(8,128)(2,1)} fusion(f32[1,22,38,512]{3,2,1,0:T(8,128)S(1)} %maximum_convert_fusion.3, f32[1,16,32,512]{3,2,1,0:T(8,128)} %copy-done.23, bf16[1,16,32,512]{3,2,1,0:T(8,128)(2,1)} %param.12, f32[512]{0:T(512)S(1)} %bitcast.397, f32[512]{0:T(512)S(1)} %bitcast.399, f32[512]{0:T(512)S(1)} %bitcast.401, ...), kind=kLoop, calls=%fused_computation.493 | loop fusion | flops 26476544 | bytes 53577728 | tf_op jit(solution)/shard_map/convert_element_type | solution.py:257
  709.0 2.3 pad_maximum_fusion.1
  711.3 5.3 copy.31
  716.7 4.0 pad_maximum_fusion
  (501 shorter events, 137.7 us)
Async XLA Ops:
  5.4 56.6 %collective-permute-start.14 = (bf16[1024,256]{1,0:T(8,128)(2,1)}, bf16[1024,256]{1,0:T(8,128)(2,1)}, u32[]{:S(2)}, u32[]{:S(2)}) collective-permute-start(bf16[1024,256]{1,0:T(8,128)(2,1)} %dynamic-slice_bitcast_fusion), channel_id=1, source_target_pairs={{0,65},{1,0},{64,1},{65,64},{2,67},{3,2},{66,3},{67,66},{4,69},{5,... | collective-permute-start | bytes 1572872 | tf_op jit(solution)/shard_map/ppermute | solution.py:33
  9.5 53.0 %collective-permute-start.6 = (bf16[1024,256]{1,0:T(8,128)(2,1)}, bf16[1024,256]{1,0:T(8,128)(2,1)}, u32[]{:S(2)}, u32[]{:S(2)}) collective-permute-start(bf16[1024,256]{1,0:T(8,128)(2,1)} %dynamic-slice_bitcast_fusion.2), channel_id=1, source_target_pairs={{0,65},{1,0},{64,1},{65,64},{2,67},{3,2},{66,3},{67,66},{4,69},{5,... | collective-permute-start | bytes 1572872 | tf_op jit(solution)/shard_map/ppermute | solution.py:33
  11.6 19.3 %collective-permute-start = (bf16[1,3,32,512]{3,2,1,0:T(8,128)(2,1)S(1)}, bf16[1,3,32,512]{3,2,1,0:T(8,128)(2,1)S(1)}, u32[]{:S(2)}, u32[]{:S(2)}) collective-permute-start(bf16[1,3,32,512]{3,2,1,0:T(8,128)(2,1)S(1)} %get-tuple-element.217), channel_id=1, source_target_pairs={{0,8},{8,16},{16,24},{24,32},{32,40},{40,48},{48,56},{56,64},{64,7... | collective-permute-start | bytes 294920 | tf_op jit(solution)/shard_map/ppermute | solution.py:58
  16.0 16.2 %collective-permute-start.1 = (bf16[1,3,32,512]{3,2,1,0:T(8,128)(2,1)}, bf16[1,3,32,512]{3,2,1,0:T(8,128)(2,1)}, u32[]{:S(2)}, u32[]{:S(2)}) collective-permute-start(bf16[1,3,32,512]{3,2,1,0:T(8,128)(2,1)} %get-tuple-element.216), channel_id=1, source_target_pairs={{8,0},{16,8},{24,16},{32,24},{40,32},{48,40},{56,48},{64,56},{72,6... | collective-permute-start | bytes 294920 | tf_op jit(solution)/shard_map/ppermute | solution.py:61
  21.3 35.3 %collective-permute-start.12 = (bf16[128,2048]{1,0:T(8,128)(2,1)}, bf16[128,2048]{1,0:T(8,128)(2,1)}, u32[]{:S(2)}, u32[]{:S(2)}) collective-permute-start(bf16[128,2048]{1,0:T(8,128)(2,1)} %dynamic-slice_bitcast_fusion.1), channel_id=1, source_target_pairs={{0,1},{1,64},{64,65},{65,0},{2,3},{3,66},{66,67},{67,2},{4,5},{5,6... | collective-permute-start | bytes 1572872 | tf_op jit(solution)/shard_map/ppermute | solution.py:32
  23.1 33.5 %copy-start.56 = (f32[1,1,512]{2,1,0:T(1,128)}, f32[1,1,512]{2,1,0:T(1,128)S(1)}, u32[]{:S(2)}) copy-start(f32[1,1,512]{2,1,0:T(1,128)S(1)} %get-tuple-element.269) | copy-start | bytes 6148
  23.1 33.5 %copy-start.58 = (f32[1,1,512]{2,1,0:T(1,128)}, f32[1,1,512]{2,1,0:T(1,128)S(1)}, u32[]{:S(2)}) copy-start(f32[1,1,512]{2,1,0:T(1,128)S(1)} %get-tuple-element.270) | copy-start | bytes 6148
  23.1 33.5 %copy-start.60 = (f32[1,1,512]{2,1,0:T(1,128)}, f32[1,1,512]{2,1,0:T(1,128)S(1)}, u32[]{:S(2)}) copy-start(f32[1,1,512]{2,1,0:T(1,128)S(1)} %get-tuple-element.271) | copy-start | bytes 6148
  23.1 33.5 %copy-start.62 = (f32[1,1,512]{2,1,0:T(1,128)}, f32[1,1,512]{2,1,0:T(1,128)S(1)}, u32[]{:S(2)}) copy-start(f32[1,1,512]{2,1,0:T(1,128)S(1)} %get-tuple-element.272) | copy-start | bytes 6148
  32.2 29.8 %copy-start = (bf16[1,19,32,512]{3,2,1,0:T(8,128)(2,1)}, bf16[1,19,32,512]{3,2,1,0:T(8,128)(2,1)S(1)}, u32[]{:S(2)}) copy-start(bf16[1,19,32,512]{3,2,1,0:T(8,128)(2,1)S(1)} %get-tuple-element.213) | copy-start | bytes 1867780
  33.3 6.1 collective-permute-start.3
  34.6 5.7 collective-permute-start.2
  39.4 21.4 %collective-permute-start.4 = (bf16[128,2048]{1,0:T(8,128)(2,1)}, bf16[128,2048]{1,0:T(8,128)(2,1)}, u32[]{:S(2)}, u32[]{:S(2)}) collective-permute-start(bf16[128,2048]{1,0:T(8,128)(2,1)} %dynamic-slice_bitcast_fusion.3), channel_id=1, source_target_pairs={{0,1},{1,64},{64,65},{65,0},{2,3},{3,66},{66,67},{67,2},{4,5},{5,6... | collective-permute-start | bytes 1572872 | tf_op jit(solution)/shard_map/ppermute | solution.py:32
  56.6 6.3 collective-permute-start.13
  60.8 3.4 collective-permute-start.5
  62.0 5.9 collective-permute-start.15
  62.5 8.2 %collective-permute-start.7 = (bf16[1024,256]{1,0:T(8,128)(2,1)}, bf16[1024,256]{1,0:T(8,128)(2,1)S(1)}, u32[]{:S(2)}, u32[]{:S(2)}) collective-permute-start(bf16[1024,256]{1,0:T(8,128)(2,1)} %collective-permute-done.6), channel_id=1, source_target_pairs={{0,8},{8,0},{1,9},{9,1},{2,10},{10,2},{3,11},{11,3},{4,12},{12,4},... | collective-permute-start | bytes 1572872 | tf_op jit(solution)/shard_map/ppermute | solution.py:24
  77.3 6.3 collective-permute-start.9
  79.6 4.9 collective-permute-start.8
  84.6 6.1 collective-permute-start.10
  88.2 5.5 collective-permute-start.11
  131.2 20.8 %collective-permute-start.17 = (bf16[1,3,32,512]{3,2,1,0:T(8,128)(2,1)}, bf16[1,3,32,512]{3,2,1,0:T(8,128)(2,1)S(1)}, u32[]{:S(2)}, u32[]{:S(2)}) collective-permute-start(bf16[1,3,32,512]{3,2,1,0:T(8,128)(2,1)} %get-tuple-element.210), channel_id=1, source_target_pairs={{8,0},{16,8},{24,16},{32,24},{40,32},{48,40},{56,48},{64,56},{72,6... | collective-permute-start | bytes 294920 | tf_op jit(solution)/shard_map/ppermute | solution.py:61
  133.1 18.9 %collective-permute-start.16 = (bf16[1,3,32,512]{3,2,1,0:T(8,128)(2,1)}, bf16[1,3,32,512]{3,2,1,0:T(8,128)(2,1)S(1)}, u32[]{:S(2)}, u32[]{:S(2)}) collective-permute-start(bf16[1,3,32,512]{3,2,1,0:T(8,128)(2,1)} %get-tuple-element.209), channel_id=1, source_target_pairs={{0,8},{8,16},{16,24},{24,32},{32,40},{40,48},{48,56},{56,64},{64,7... | collective-permute-start | bytes 294920 | tf_op jit(solution)/shard_map/ppermute | solution.py:58
  140.3 108.7 %collective-permute-start.26 = (bf16[512,2,1024]{2,0,1:T(8,128)(2,1)}, bf16[512,2,1024]{2,0,1:T(8,128)(2,1)}, u32[]{:S(2)}, u32[]{:S(2)}) collective-permute-start(bf16[512,2,1024]{2,0,1:T(8,128)(2,1)} %fusion.18), channel_id=1, source_target_pairs={{0,8},{8,0},{1,9},{9,1},{2,10},{10,2},{3,11},{11,3},{4,12},{12,4},... | collective-permute-start | bytes 6291464 | tf_op jit(solution)/shard_map/ppermute | solution.py:24
  153.1 30.2 %collective-permute-start.19 = (bf16[1,22,3,512]{3,2,1,0:T(4,128)(2,1)S(1)}, bf16[1,22,3,512]{3,2,1,0:T(4,128)(2,1)S(1)}, u32[]{:S(2)}, u32[]{:S(2)}) collective-permute-start(bf16[1,22,3,512]{3,2,1,0:T(4,128)(2,1)S(1)} %get-tuple-element.198), channel_id=1, source_target_pairs={{2,0},{4,2},{6,4},{3,1},{5,3},{7,5},{10,8},{12,10},{14,12},{11,9},... | collective-permute-start | bytes 202760 | tf_op jit(solution)/shard_map/ppermute | solution.py:61
  154.4 28.9 %collective-permute-start.18 = (bf16[1,22,3,512]{3,2,1,0:T(4,128)(2,1)S(1)}, bf16[1,22,3,512]{3,2,1,0:T(4,128)(2,1)S(1)}, u32[]{:S(2)}, u32[]{:S(2)}) collective-permute-start(bf16[1,22,3,512]{3,2,1,0:T(4,128)(2,1)S(1)} %get-tuple-element.197), channel_id=1, source_target_pairs={{0,2},{2,4},{4,6},{1,3},{3,5},{5,7},{8,10},{10,12},{12,14},{9,11},... | collective-permute-start | bytes 202760 | tf_op jit(solution)/shard_map/ppermute | solution.py:58
  158.5 36.6 %copy-start.52 = (bf16[7,7,512]{2,1,0:T(8,128)(2,1)}, bf16[7,7,512]{2,1,0:T(8,128)(2,1)S(1)}, u32[]{:S(2)}) copy-start(bf16[7,7,512]{2,1,0:T(8,128)(2,1)S(1)} %constant_dynamic-update-slice_fusion.18) | copy-start | bytes 150532
  209.6 55.0 %collective-permute-start.24 = (bf16[512,2,1024]{2,0,1:T(8,128)(2,1)}, bf16[512,2,1024]{2,0,1:T(8,128)(2,1)}, u32[]{:S(2)}, u32[]{:S(2)}) collective-permute-start(bf16[512,2,1024]{2,0,1:T(8,128)(2,1)} %fusion.20), channel_id=1, source_target_pairs={{0,8},{8,0},{1,9},{9,1},{2,10},{10,2},{3,11},{11,3},{4,12},{12,4},... | collective-permute-start | bytes 6291464 | tf_op jit(solution)/shard_map/ppermute | solution.py:24
  234.5 24.4 %all-to-all-start.4 = ((bf16[128,2,256]{2,1,0:T(2,128)(2,1)}), bf16[128,2,256]{2,1,0:T(2,128)(2,1)S(1)}, u32[]{:S(2)}, u32[]{:S(2)}) async-start(bf16[128,2,256]{2,1,0:T(2,128)(2,1)} %reshape.941), calls=%async_computation.4 | async-start | bytes 262144 | tf_op jit(solution)/shard_map/all_to_all | solution.py:184
  258.9 32.8 %all-to-all-start.2 = ((bf16[64,8,2,1024]{3,1,2,0:T(8,128)(2,1)}), bf16[64,8,2,1024]{3,1,2,0:T(8,128)(2,1)}, u32[]{:S(2)}, u32[]{:S(2)}) async-start(bf16[64,8,2,1024]{3,1,2,0:T(8,128)(2,1)} %copy.28), calls=%async_computation.2 | async-start | bytes 4194304 | tf_op jit(solution)/shard_map/all_to_all | solution.py:166
  291.7 33.7 %all-to-all-start = ((bf16[64,8,2,1024]{3,1,2,0:T(8,128)(2,1)}), bf16[64,8,2,1024]{3,1,2,0:T(8,128)(2,1)}, u32[]{:S(2)}, u32[]{:S(2)}) async-start(bf16[64,8,2,1024]{3,1,2,0:T(8,128)(2,1)} %copy.26), calls=%async_computation | async-start | bytes 4194304 | tf_op jit(solution)/shard_map/all_to_all | solution.py:166
  326.4 23.8 %all-to-all-start.3 = ((bf16[32,8,2,1024]{3,1,2,0:T(8,128)(2,1)}), bf16[32,8,2,1024]{3,1,2,0:T(8,128)(2,1)S(1)}, u32[]{:S(2)}, u32[]{:S(2)}) async-start(bf16[32,8,2,1024]{3,1,2,0:T(8,128)(2,1)} %broadcast_in_dim.7), calls=%async_computation.3 | async-start | bytes 2097152 | tf_op jit(solution)/shard_map/all_to_all | solution.py:169
  334.9 337.1 %copy-start.20 = (bf16[1,16,32,512]{3,2,1,0:T(8,128)(2,1)}, bf16[1,16,32,512]{3,2,1,0:T(8,128)(2,1)S(1)}, u32[]{:S(2)}) copy-start(bf16[1,16,32,512]{3,2,1,0:T(8,128)(2,1)S(1)} %convert_element_type.643) | copy-start | bytes 1572868
  351.4 341.6 %all-to-all-start.1 = ((bf16[32,8,2,1024]{3,1,2,0:T(8,128)(2,1)}), bf16[32,8,2,1024]{3,1,2,0:T(8,128)(2,1)}, u32[]{:S(2)}, u32[]{:S(2)}) async-start(bf16[32,8,2,1024]{3,1,2,0:T(8,128)(2,1)} %broadcast_in_dim.6), calls=%async_computation.1 | async-start | bytes 2097152 | tf_op jit(solution)/shard_map/all_to_all | solution.py:169
  357.6 14.2 %collective-permute-start.21 = (bf16[1,3,32,512]{3,2,1,0:T(8,128)(2,1)S(1)}, bf16[1,3,32,512]{3,2,1,0:T(8,128)(2,1)S(1)}, u32[]{:S(2)}, u32[]{:S(2)}) collective-permute-start(bf16[1,3,32,512]{3,2,1,0:T(8,128)(2,1)S(1)} %get-tuple-element.208), channel_id=1, source_target_pairs={{8,0},{16,8},{24,16},{32,24},{40,32},{48,40},{56,48},{64,56},{72,6... | collective-permute-start | bytes 294920 | tf_op jit(solution)/shard_map/ppermute | solution.py:61
  361.8 10.0 %collective-permute-start.20 = (bf16[1,3,32,512]{3,2,1,0:T(8,128)(2,1)S(1)}, bf16[1,3,32,512]{3,2,1,0:T(8,128)(2,1)S(1)}, u32[]{:S(2)}, u32[]{:S(2)}) collective-permute-start(bf16[1,3,32,512]{3,2,1,0:T(8,128)(2,1)S(1)} %get-tuple-element.207), channel_id=1, source_target_pairs={{0,8},{8,16},{16,24},{24,32},{32,40},{40,48},{48,56},{56,64},{64,7... | collective-permute-start | bytes 294920 | tf_op jit(solution)/shard_map/ppermute | solution.py:58
  371.9 302.3 %collective-permute-start.23 = (bf16[1,22,3,512]{3,2,1,0:T(4,128)(2,1)S(1)}, bf16[1,22,3,512]{3,2,1,0:T(4,128)(2,1)S(1)}, u32[]{:S(2)}, u32[]{:S(2)}) collective-permute-start(bf16[1,22,3,512]{3,2,1,0:T(4,128)(2,1)S(1)} %get-tuple-element.196), channel_id=1, source_target_pairs={{2,0},{4,2},{6,4},{3,1},{5,3},{7,5},{10,8},{12,10},{14,12},{11,9},... | collective-permute-start | bytes 202760 | tf_op jit(solution)/shard_map/ppermute | solution.py:61
  373.2 301.0 %collective-permute-start.22 = (bf16[1,22,3,512]{3,2,1,0:T(4,128)(2,1)S(1)}, bf16[1,22,3,512]{3,2,1,0:T(4,128)(2,1)S(1)}, u32[]{:S(2)}, u32[]{:S(2)}) collective-permute-start(bf16[1,22,3,512]{3,2,1,0:T(4,128)(2,1)S(1)} %get-tuple-element.195), channel_id=1, source_target_pairs={{0,2},{2,4},{4,6},{1,3},{3,5},{5,7},{8,10},{10,12},{12,14},{9,11},... | collective-permute-start | bytes 202760 | tf_op jit(solution)/shard_map/ppermute | solution.py:58
  671.4 23.0 %copy-start.57 = (f32[1,1,512]{2,1,0:T(1,128)S(1)}, f32[1,1,512]{2,1,0:T(1,128)}, u32[]{:S(2)}) copy-start(f32[1,1,512]{2,1,0:T(1,128)} %copy-done.56) | copy-start | bytes 6148
  671.4 23.0 %copy-start.59 = (f32[1,1,512]{2,1,0:T(1,128)S(1)}, f32[1,1,512]{2,1,0:T(1,128)}, u32[]{:S(2)}) copy-start(f32[1,1,512]{2,1,0:T(1,128)} %copy-done.58) | copy-start | bytes 6148
  671.4 23.0 %copy-start.61 = (f32[1,1,512]{2,1,0:T(1,128)S(1)}, f32[1,1,512]{2,1,0:T(1,128)}, u32[]{:S(2)}) copy-start(f32[1,1,512]{2,1,0:T(1,128)} %copy-done.60) | copy-start | bytes 6148
  671.4 23.0 %copy-start.63 = (f32[1,1,512]{2,1,0:T(1,128)S(1)}, f32[1,1,512]{2,1,0:T(1,128)}, u32[]{:S(2)}) copy-start(f32[1,1,512]{2,1,0:T(1,128)} %copy-done.62) | copy-start | bytes 6148
  671.4 23.0 %copy-start.64 = (f32[1,1,512]{2,1,0:T(1,128)S(1)}, f32[1,1,512]{2,1,0:T(1,128)}, u32[]{:S(2)}) copy-start(f32[1,1,512]{2,1,0:T(1,128)} %get-tuple-element.273) | copy-start | bytes 6148
  671.4 23.0 %copy-start.65 = (f32[1,1,512]{2,1,0:T(1,128)S(1)}, f32[1,1,512]{2,1,0:T(1,128)}, u32[]{:S(2)}) copy-start(f32[1,1,512]{2,1,0:T(1,128)} %get-tuple-element.274) | copy-start | bytes 6148
  671.4 23.0 %copy-start.66 = (f32[1,1,512]{2,1,0:T(1,128)S(1)}, f32[1,1,512]{2,1,0:T(1,128)}, u32[]{:S(2)}) copy-start(f32[1,1,512]{2,1,0:T(1,128)} %get-tuple-element.275) | copy-start | bytes 6148
  671.4 23.0 %copy-start.67 = (f32[1,1,512]{2,1,0:T(1,128)S(1)}, f32[1,1,512]{2,1,0:T(1,128)}, u32[]{:S(2)}) copy-start(f32[1,1,512]{2,1,0:T(1,128)} %get-tuple-element.276) | copy-start | bytes 6148
  676.6 27.3 %collective-permute-start.27 = (bf16[256,2,1024]{2,0,1:T(8,128)(2,1)}, bf16[256,2,1024]{2,0,1:T(8,128)(2,1)}, u32[]{:S(2)}, u32[]{:S(2)}) collective-permute-start(bf16[256,2,1024]{2,0,1:T(8,128)(2,1)} %bitcast.371), channel_id=1, source_target_pairs={{0,8},{8,0},{1,9},{9,1},{2,10},{10,2},{3,11},{11,3},{4,12},{12,4},... | collective-permute-start | bytes 3145736 | tf_op jit(solution)/shard_map/ppermute | solution.py:24
  694.3 9.6 %collective-permute-start.25 = (bf16[256,2,1024]{2,0,1:T(8,128)(2,1)S(1)}, bf16[256,2,1024]{2,0,1:T(8,128)(2,1)S(1)}, u32[]{:S(2)}, u32[]{:S(2)}) collective-permute-start(bf16[256,2,1024]{2,0,1:T(8,128)(2,1)S(1)} %bitcast.382), channel_id=1, source_target_pairs={{0,8},{8,0},{1,9},{9,1},{2,10},{10,2},{3,11},{11,3},{4,12},{12,4},... | collective-permute-start | bytes 3145736 | tf_op jit(solution)/shard_map/ppermute | solution.py:24
  (93 other events, 882.9 us)
